TPU v7x, 32 devices: a whole 2x2x4 slice. The times are simulated.
32 devices in a mesh: prow: 4 (over y, core), pcol: 8 (over z, x).
Axes of the slice: x: 2, y: 2, z: 4, core: 2. Of those that a mesh axis runs over, the one named last changes fastest.
Arguments:
- tiles: bfloat16 [4, 8, 16, 256, 256], P('prow', 'pcol'), may hold values from -6 to 6
- tile_ids: int32 [4, 8, 16], P('prow', 'pcol'), may hold values from 0 to 127, as said below
- counts: int32 [4, 8], P('prow', 'pcol'), may hold values from 1 to 16, as said below
- pivots: int32 [256], replicated, may hold values from 0 to 16383, as said below
- l_inverse: bfloat16 [256, 256], P(None, 'pcol'), may hold values from -1 to 1, as said below
- u_inverse: bfloat16 [256, 256], P('prow'), may hold values from -0.125 to 0.5, as said below
Outputs:
- factored: bfloat16 [4, 8, 16, 256, 256], P('prow', 'pcol')
Inputs may be any that keep to these rules, and one draw needn't show every extreme that they name: Live slot s of device (p, q) holds local tile row tile_ids[p, q, s] // 8 and local tile column tile_ids[p, q, s] % 8; live codes of one device are distinct, padded slots hold arbitrary codes. Let R be the tile rows I >= 1 with tile (I, 0) held and C the tile columns J >= 1 with tile (0, J) held. Tile (0, 0) is held; on each prow index R takes the last one to 3 local tile rows, on each pcol index C takes the last one to 3 local tile columns, and both most counts are reached on some index. Every tile whose row is 0 or in R and whose column is 0 or in C is held; no other held tile lies in tile row 0, a tile row of R, or tile column 0. `counts`: some device has 16 live slots. Row r of tile row 0 and row pivots[r] change places; pivots[r] is r or a row of a tile row of R, and the values that differ from their r are distinct. `l_inverse`: lower triangular with unit diagonal. `u_inverse`: upper triangular with a positive diagonal.
All inputs are finite; a program needn't handle non-finite values.
Results may differ from a plain program's by a relative error of at most 0.0056.
Values may be sent and summed in bfloat16 or wider, within the bound.
A program may use at most 64 MiB of HBM per device.

v0:
```python
import jax
import jax.numpy as jnp
from jax import lax
from jax.sharding import PartitionSpec as P

TILE_SIDE = 256
LOCAL_ROWS = 16
TILE_SLOTS = 16
LOWER_MOST = 3
UPPER_MOST = 3


def broadcast(value, axis, source):
    kept = jnp.where(lax.axis_index(axis) == source, value, 0).astype(value.dtype)
    return lax.psum(kept, axis)


def pick_rows(tile, rows):
    return tile[rows]


def body(tiles, tile_ids, counts, pivots, l_inverse, u_inverse):
    row_count = lax.axis_size("prow")
    col_count = lax.axis_size("pcol")
    my_row = lax.axis_index("prow")
    my_col = lax.axis_index("pcol")
    grid_cols = LOCAL_ROWS * row_count // col_count
    total_rows = LOCAL_ROWS * row_count * TILE_SIDE
    local = tiles[0, 0]
    codes = tile_ids[0, 0]
    slot_range = jnp.arange(TILE_SLOTS, dtype=jnp.int32)
    alive = slot_range < counts[0, 0]
    loc_row = codes // grid_cols
    loc_col = codes % grid_cols
    glob_row = my_row + row_count * loc_row
    glob_col = my_col + col_count * loc_col
    col_range = jnp.arange(grid_cols, dtype=jnp.int32)
    upper_inv = lax.all_gather(u_inverse, "prow", axis=0, tiled=True)
    lower_inv = lax.all_gather(l_inverse, "pcol", axis=1, tiled=True)
    source_tile = pivots // TILE_SIDE
    source_row = pivots % TILE_SIDE
    gathered = local[:, source_row, :]
    owned = (source_tile[None, :] == glob_row[:, None]) & alive[:, None]
    contrib = jnp.where(owned[:, :, None], gathered, jnp.zeros_like(gathered))
    col_hot = ((loc_col[:, None] == col_range[None, :]) & alive[:, None]).astype(jnp.bfloat16)
    top_flag = (glob_row == 0).astype(jnp.bfloat16)
    top_hot = col_hot * top_flag[:, None]
    flag_part = jnp.sum(
        top_hot.astype(jnp.float32) * (glob_col >= 1).astype(jnp.float32)[:, None], axis=0
    )
    new_part = jnp.einsum("sj,srb->jrb", col_hot, contrib, preferred_element_type=jnp.float32)
    old_part = jnp.einsum("sj,srb->jrb", top_hot, local, preferred_element_type=jnp.float32)
    new_sum, old_sum, flag_sum = (
        lax.psum(new_part.astype(jnp.bfloat16), "prow").astype(jnp.float32),
        lax.psum(old_part.astype(jnp.bfloat16), "prow").astype(jnp.float32),
        lax.psum(flag_part.astype(jnp.bfloat16), "prow").astype(jnp.float32),
    )
    new_top = new_sum.astype(jnp.bfloat16)
    old_top = old_sum.astype(jnp.bfloat16)
    anchor_top = (
        jnp.full((total_rows,), -1, jnp.int32)
        .at[pivots]
        .set(jnp.arange(TILE_SIDE, dtype=jnp.int32))
    )
    row_index = glob_row[:, None] * TILE_SIDE + jnp.arange(TILE_SIDE, dtype=jnp.int32)[None, :]
    anchor = anchor_top[row_index]
    moved = (anchor >= 0) & (glob_row >= 1)[:, None]
    from_top = jax.vmap(pick_rows)(old_top[loc_col], jnp.maximum(anchor, 0))
    swapped = jnp.where(moved[:, :, None], from_top, local)
    primed = jnp.where((glob_row == 0)[:, None, None], new_top[loc_col], swapped)
    panel_mask = alive & (glob_col == 0) & (glob_row >= 1)
    panel_slots = jnp.argsort(jnp.where(panel_mask, 0, 1), stable=True)[:LOWER_MOST]
    panel_valid = panel_mask[panel_slots]
    lower_full = jnp.einsum(
        "kab,bc->kac", primed[panel_slots], upper_inv, preferred_element_type=jnp.float32
    )
    lower_list = jnp.where(panel_valid[:, None, None], lower_full, 0.0).astype(jnp.bfloat16)
    lower_rows = jnp.where(panel_valid, loc_row[panel_slots], -1)
    got_list, got_rows = (broadcast(lower_list, "pcol", 0), broadcast(lower_rows, "pcol", 0))
    row_match = got_rows[None, :] == loc_row[:, None]
    lower_pick = jnp.sum(
        jnp.where(row_match, jnp.arange(LOWER_MOST, dtype=jnp.int32)[None, :], 0), axis=1
    )
    lower_present = jnp.any(row_match, axis=1)
    column_flags = flag_sum > 0.5
    column_order = jnp.argsort(jnp.where(column_flags, 0, 1), stable=True)[:UPPER_MOST]
    upper_valid = column_flags[column_order]
    upper_full = jnp.einsum(
        "ab,kbc->kac", lower_inv, new_top[column_order], preferred_element_type=jnp.float32
    )
    upper_list = jnp.where(upper_valid[:, None, None], upper_full, 0.0).astype(jnp.bfloat16)
    upper_ids = jnp.where(upper_valid, column_order, -1)
    col_match = upper_ids[None, :] == loc_col[:, None]
    upper_pick = jnp.sum(
        jnp.where(col_match, jnp.arange(UPPER_MOST, dtype=jnp.int32)[None, :], 0), axis=1
    )
    upper_present = jnp.any(col_match, axis=1)
    result = jnp.where(alive[:, None, None], primed, jnp.zeros_like(primed))
    upper_mask = alive & (glob_row == 0) & (glob_col >= 1)
    result = jnp.where(upper_mask[:, None, None], upper_list[upper_pick], result)
    result = result.at[panel_slots].set(
        jnp.where(panel_valid[:, None, None], lower_list, result[panel_slots])
    )
    needs = alive & (glob_row >= 1) & (glob_col >= 1) & lower_present & upper_present
    order = jnp.argsort(jnp.where(needs, 0, 1), stable=True)
    needed = jnp.sum(needs.astype(jnp.int32))

    def trailing(current, lower_tile, upper_index):
        product = jnp.dot(lower_tile, upper_list[upper_index], preferred_element_type=jnp.float32)
        return (current.astype(jnp.float32) - product).astype(jnp.bfloat16)

    def own_step(position, held):
        slot = order[position]
        value = trailing(primed[slot], got_list[lower_pick[slot]], upper_pick[slot])
        return held.at[slot].set(value)

    result = lax.fori_loop(0, needed, own_step, result)
    return result[None, None]


def solution(mesh):
    placed = (
        P("prow", "pcol", None, None, None),
        P("prow", "pcol", None),
        P("prow", "pcol"),
        P(),
        P(None, "pcol"),
        P("prow", None),
    )
    return jax.shard_map(
        body,
        mesh=mesh,
        in_specs=placed,
        out_specs=P("prow", "pcol", None, None, None),
        check_vma=False,
    )
```

profile of v0, /device:TPU:0, one launch (start us, length us, event | category | flops | bytes accessed | tf_op | source)
XLA Modules:
  0.0 367.1 jit_solution(17851985653120215926)
XLA Ops:
  7.2 2.9 copy.87
  10.2 2.2 convolution_convert_fusion
  12.8 2.1 gather_fusion.1
  14.9 3.0 fusion.11
  17.9 8.4 %psum.35 = bf16[8]{0:T(256)(128)(2,1)S(1)} all-reduce(bf16[8]{0:T(256)(128)(2,1)S(1)} %multiply_reduce_fusion), channel_id=1, replica_groups=mesh['prow'=4,'pcol'=8] {'prow'}, use_global_device_ids=true, to_apply=%region_1.2 | all-reduce | flops 8 | bytes 32 | tf_op jit(solution)/shard_map/psum | solution.py:56
  30.6 11.6 %psum.38 = s32[3]{0:T(128)S(1)} all-reduce(s32[3]{0:T(128)S(1)} %broadcast_select_fusion.2), channel_id=1, replica_groups=mesh['prow'=4,'pcol'=8] {'pcol'}, use_global_device_ids=true, to_apply=%region_9.10 | all-reduce | flops 3 | bytes 24 | tf_op jit(solution)/shard_map/psum | solution.py:15
  42.5 1.4 scatter_custom_fusion
  43.9 23.0 %gather_fusion.5 = s32[4096]{0:T(1024)S(1)} fusion(s32[16384]{0:T(1024)S(1)} %scatter_custom_fusion, s32[4096]{0:T(1024)S(1)} %broadcast_clamp_fusion), kind=kCustom, calls=%fused_computation.5 | custom fusion | bytes 49152 | tf_op jit(solution)/shard_map/gather | solution.py:66
  67.3 6.0 %all_gather.7 = bf16[256,256]{1,0:T(8,128)(2,1)S(1)} all-gather(bf16[64,256]{1,0:T(8,128)(2,1)S(1)} %copy-done.4), channel_id=1, replica_groups=mesh['prow'=4,'pcol'=8] {'prow'}, dimensions={0}, use_global_device_ids=true | all-gather | bytes 163840 | tf_op jit(solution)/shard_map/all_gather | solution.py:38
  73.2 30.7 %all_gather.6 = bf16[256,256]{0,1:T(8,128)(2,1)S(1)} all-gather(bf16[256,32]{0,1:T(8,128)(2,1)S(1)} %copy-done.5), channel_id=1, replica_groups=mesh['prow'=4,'pcol'=8] {'pcol'}, dimensions={1}, use_global_device_ids=true | all-gather | bytes 147456 | tf_op jit(solution)/shard_map/all_gather | solution.py:39
  104.1 1.5 copy.63
  105.9 1.3 gather_fusion.2
  107.2 2.0 gather_fusion.4
  111.4 40.7 %gather_fusion.11 = bf16[4096,256]{1,0:T(8,128)(2,1)} fusion(bf16[16,256,256]{2,1,0:T(8,128)(2,1)S(1)} %gather_fusion.6, s32[4096]{0:T(1024)S(1)} %bitcast.105), kind=kCustom, calls=%fused_computation.11 | custom fusion | bytes 4227072 | tf_op jit(solution)/shard_map/vmap()/gather | solution.py:19
  152.1 2.0 gather_fusion.3
  154.1 16.0 %copy_select_fusion = (bf16[16,256,256]{2,0,1:T(8,128)(2,1)}, bf16[16,256,256]{2,0,1:T(8,128)(2,1)S(1)}) fusion(bf16[16,256,256]{2,1,0:T(8,128)(2,1)} %gather_fusion.3, pred[16]{0:T(512)(128)(4,1)S(1)} %iota_compare_fusion.1, pred[16]{0:T(512)(128)(4,1)S(1)} %get-tuple-element.155, bf16[1,1,16,256,256]{4,3,2,1,0:T(8,128)(2,1)S(1)} %copy-done.1, ...), kind=kLoop, calls=%fused_computation.27 | loop fusion | flops 4194304 | bytes 12587056 | tf_op jit(solution)/shard_map/jit(_where)/select_n | solution.py:100
  170.1 2.1 copy.67
  172.2 2.2 gather_fusion.8
  174.4 2.1 copy.69
  176.5 2.2 gather_fusion.9
  181.8 2.4 scatter_fusion
  184.2 64.8 %all-reduce.4.cloned.1.call-done = bf16[3,256,256]{2,1,0:T(8,128)(2,1)} async-done(((bf16[3,256,256]{2,1,0:T(8,128)(2,1)}), bf16[3,256,256]{2,1,0:T(8,128)(2,1)}) %all-reduce.4.cloned.1.call-update) | async-done | bytes 393232 | tf_op jit(solution)/shard_map/psum | solution.py:15
  249.0 111.2 %while.11 = (s32[]{:T(128)}, bf16[16,256,256]{2,1,0:T(8,128)(2,1)}, s32[]{:T(128)}, s32[16]{0:T(128)S(1)}, bf16[16,256,256]{2,1,0:T(8,128)(2,1)}, /*index=5*/s32...) while((s32[]{:T(128)}, bf16[16,256,256]{2,1,0:T(8,128)(2,1)}, ...), condition=%wide.region_18.19_spmd, body=%wide.region_16.18_spmd.sunk | while | flops 33816608 | bytes 656726 | solution.py:117
  258.7 2.6 fusion.49
  271.0 2.6 fusion.49
  283.3 2.6 fusion.49
  295.5 2.6 fusion.49
  307.8 2.6 fusion.49
  320.1 2.6 fusion.49
  332.4 2.6 fusion.49
  344.7 2.6 fusion.49
  356.9 2.6 fusion.49
  (111 shorter events, 36.0 us)
Async XLA Ops:
  6.5 97.5 %all-reduce.6.cloned.1.call-start = ((), (), s32[]{:S(2)}) async-start(), calls=%async_computation.1 | async-start | bytes 4194304 | tf_op jit(solution)/shard_map/psum | solution.py:54
  7.2 3.0 copy-start.8
  7.2 3.0 copy-start
  10.1 2.4 copy-start.7
  17.9 231.1 %all-reduce.4.cloned.1.call-start = ((), (), s32[]{:S(2)}) async-start(), calls=%async_computation | async-start | bytes 786432 | tf_op jit(solution)/shard_map/psum | solution.py:15
  43.9 23.4 %copy-start.4 = (bf16[64,256]{1,0:T(8,128)(2,1)S(1)}, bf16[64,256]{1,0:T(8,128)(2,1)}, u32[]{:S(2)}) copy-start(bf16[64,256]{1,0:T(8,128)(2,1)} %param.15) | copy-start | bytes 98308
  43.9 29.3 %copy-start.5 = (bf16[256,32]{0,1:T(8,128)(2,1)S(1)}, bf16[256,32]{0,1:T(8,128)(2,1)}, u32[]{:S(2)}) copy-start(bf16[256,32]{0,1:T(8,128)(2,1)} %param.14) | copy-start | bytes 49156
  104.1 1.5 copy-start.3
  152.1 2.0 copy-start.1
  170.1 4.3 %copy-start.2 = (bf16[16,256,256]{2,0,1:T(8,128)(2,1)S(1)}, bf16[16,256,256]{2,0,1:T(8,128)(2,1)}, u32[]{:S(2)}) copy-start(bf16[16,256,256]{2,0,1:T(8,128)(2,1)} %get-tuple-element.145) | copy-start | bytes 6291460
  176.5 72.5 %copy-start.6 = (s32[3]{0:T(128)S(1)}, s32[3]{0:T(128)}, u32[]{:S(2)}) copy-start(s32[3]{0:T(128)} %constant.108.clone.1) | copy-start | bytes 40
Sparse Core Ops, SparseCore 0:
  18.0 54.8 all-reduce.5
  179.8 69.1 all-reduce.3
where the time goes:
time: 369 us; the launch traced here: 367 us
  local copies, waits for them, and re-layouts  109 us (30%)
  waiting for transfers between devices  64.8 us (18%)
  loops' own time  62.9 us (17%)
  blocking collectives  56.7 us (15%)
  matrix products  30.7 us (8%)
  other arithmetic  28.2 us (8%)
  between operations  14.4 us (4%)
    psum x1, waiting for transfers between devices, broadcast(): return lax.psum(kept, axis)  64.8 us
    another operation x1, loops' own time, body(): result = lax.fori_loop(0, needed, own_step, result)  62.9 us
    gather x2, local copies, waits for them, and re-layouts, pick_rows(): return tile[rows]  40.7 us
    all_gather x1, blocking collectives, body(): lower_inv = lax.all_gather(l_inverse, 'pcol', axis=1, tiled=True)  30.7 us
    dot_general x9, matrix products, trailing(): jnp.dot(lower_tile, upper_list[upper_index], preferred_element_type=jnp.f...  23.2 us
    gather x1, local copies, waits for them, and re-layouts, body(): anchor = anchor_top[row_index]  23 us
    select_n x1, other arithmetic, body(): jnp.where(upper_mask[:, None, None], upper_list[upper_pick], result)  16 us
    dynamic_slice x18, local copies, waits for them, and re-layouts, own_step(): value = trailing(primed[slot], got_list[lower_pick[slot]], upper_pick[slot])  12.1 us
  transfers between devices with their start and end apart: 2, of which 1 were waited for; matrix products, arithmetic and copies ran while one was open for 9% of the time, Pallas kernels for 0%

commit v1 on v0

--- a/solution.py
+++ b/solution.py
@@ -36,7 +36,12 @@
     glob_col = my_col + col_count * loc_col
     col_range = jnp.arange(grid_cols, dtype=jnp.int32)
     upper_inv = lax.all_gather(u_inverse, "prow", axis=0, tiled=True)
-    lower_inv = lax.all_gather(l_inverse, "pcol", axis=1, tiled=True)
+    ring = [l_inverse]
+    for hop in range(7):
+        ring.append(lax.ppermute(ring[-1], "pcol", [(dev, (dev + 1) % 8) for dev in range(8)]))
+    lower_inv = jnp.roll(
+        jnp.concatenate(ring[::-1], axis=1), (lax.axis_index("pcol") + 1) * ring[0].shape[1], axis=1
+    )
     source_tile = pivots // TILE_SIDE
     source_row = pivots % TILE_SIDE
     gathered = local[:, source_row, :]

time: 369 us -> 379 us (1.027)
  waiting for transfers between devices: 64.8 us -> 103 us
  blocking collectives: 56.7 us -> 24 us
    ppermute x0 -> x7, waiting for transfers between devices: none -> 35.5 us  [body(): lax.ppermute(ring[-1], 'pcol', [(dev, (dev + 1) % 8) for dev in range(8)])]
    all_gather x1 -> x0, blocking collectives: 30.7 us -> none  [body(): lower_inv = lax.all_gather(l_inverse, 'pcol', axis=1, tiled=True)]
  transfers between devices with their start and end apart: 2 -> 9, of which waited for: 1 -> 7; matrix products, arithmetic and copies ran while one was open for 9% -> 12% of each run, Pallas kernels for 0% -> 0%
where the time goes in v1:
time: 379 us; the launch traced here: 378 us
  local copies, waits for them, and re-layouts  111 us (29%)
  waiting for transfers between devices  103 us (27%)
  loops' own time  62.9 us (17%)
  matrix products  30.8 us (8%)
  other arithmetic  28.2 us (7%)
  blocking collectives  24 us (6%)
  between operations  14.4 us (4%)
    psum x1, waiting for transfers between devices, broadcast(): return lax.psum(kept, axis)  67.9 us
    another operation x1, loops' own time, body(): result = lax.fori_loop(0, needed, own_step, result)  62.9 us
    gather x2, local copies, waits for them, and re-layouts, pick_rows(): return tile[rows]  40.7 us
    ppermute x7, waiting for transfers between devices, body(): lax.ppermute(ring[-1], 'pcol', [(dev, (dev + 1) % 8) for dev in range(8)])  35.5 us
    dot_general x9, matrix products, trailing(): jnp.dot(lower_tile, upper_list[upper_index], preferred_element_type=jnp.f...  23.2 us
    gather x1, local copies, waits for them, and re-layouts, body(): anchor = anchor_top[row_index]  23 us
    select_n x1, other arithmetic, body(): jnp.where(upper_mask[:, None, None], upper_list[upper_pick], result)  16 us
    dynamic_slice x18, local copies, waits for them, and re-layouts, own_step(): value = trailing(primed[slot], got_list[lower_pick[slot]], upper_pick[slot])  12.1 us
  transfers between devices with their start and end apart: 9, of which 7 were waited for; matrix products, arithmetic and copies ran while one was open for 12% of the time, Pallas kernels for 0%

profile of v1, /device:TPU:0, one launch (start us, length us, event | category | flops | bytes accessed | tf_op | source)
XLA Modules:
  0.0 377.8 jit_solution(14765433759952903598)
XLA Ops:
  7.4 3.0 collective-permute-start
  11.1 2.9 copy.102
  14.1 2.2 convolution_convert_fusion
  16.7 2.1 gather_fusion.1
  18.7 3.0 fusion.11
  21.8 6.3 %psum.35 = bf16[8]{0:T(256)(128)(2,1)S(1)} all-reduce(bf16[8]{0:T(256)(128)(2,1)S(1)} %multiply_reduce_fusion), channel_id=1, replica_groups=mesh['prow'=4,'pcol'=8] {'prow'}, use_global_device_ids=true, to_apply=%region_1.2 | all-reduce | flops 8 | bytes 32 | tf_op jit(solution)/shard_map/psum | solution.py:61
  32.4 11.6 %psum.38 = s32[3]{0:T(128)S(1)} all-reduce(s32[3]{0:T(128)S(1)} %broadcast_select_fusion.2), channel_id=1, replica_groups=mesh['prow'=4,'pcol'=8] {'pcol'}, use_global_device_ids=true, to_apply=%region_9.10 | all-reduce | flops 3 | bytes 24 | tf_op jit(solution)/shard_map/psum | solution.py:15
  45.7 23.0 %gather_fusion.5 = s32[4096]{0:T(1024)S(1)} fusion(s32[16384]{0:T(1024)S(1)} %scatter_custom_fusion, s32[4096]{0:T(1024)S(1)} %broadcast_clamp_fusion), kind=kCustom, calls=%fused_computation.5 | custom fusion | bytes 49152 | tf_op jit(solution)/shard_map/gather | solution.py:71
  69.2 6.7 %collective-permute-done.1 = bf16[256,32]{1,0:T(8,128)(2,1)S(1)} collective-permute-done((bf16[256,32]{1,0:T(8,128)(2,1)S(1)}, bf16[256,32]{1,0:T(8,128)(2,1)S(1)}, u32[]{:S(2)}, u32[]{:S(2)}) %collective-permute-start.1) | collective-permute-done | bytes 16416 | tf_op jit(solution)/shard_map/ppermute | solution.py:41
  76.0 6.9 %collective-permute-done.2 = bf16[256,32]{1,0:T(8,128)(2,1)S(1)} collective-permute-done((bf16[256,32]{1,0:T(8,128)(2,1)S(1)}, bf16[256,32]{1,0:T(8,128)(2,1)S(1)}, u32[]{:S(2)}, u32[]{:S(2)}) %collective-permute-start.2) | collective-permute-done | bytes 16416 | tf_op jit(solution)/shard_map/ppermute | solution.py:41
  82.8 7.3 %collective-permute-done.3 = bf16[256,32]{1,0:T(8,128)(2,1)S(1)} collective-permute-done((bf16[256,32]{1,0:T(8,128)(2,1)S(1)}, bf16[256,32]{1,0:T(8,128)(2,1)S(1)}, u32[]{:S(2)}, u32[]{:S(2)}) %collective-permute-start.3) | collective-permute-done | bytes 16416 | tf_op jit(solution)/shard_map/ppermute | solution.py:41
  90.2 7.0 %collective-permute-done.4 = bf16[256,32]{1,0:T(8,128)(2,1)S(1)} collective-permute-done((bf16[256,32]{1,0:T(8,128)(2,1)S(1)}, bf16[256,32]{1,0:T(8,128)(2,1)S(1)}, u32[]{:S(2)}, u32[]{:S(2)}) %collective-permute-start.4) | collective-permute-done | bytes 16416 | tf_op jit(solution)/shard_map/ppermute | solution.py:41
  97.1 7.0 %collective-permute-done.5 = bf16[256,32]{1,0:T(8,128)(2,1)S(1)} collective-permute-done((bf16[256,32]{1,0:T(8,128)(2,1)S(1)}, bf16[256,32]{1,0:T(8,128)(2,1)S(1)}, u32[]{:S(2)}, u32[]{:S(2)}) %collective-permute-start.5) | collective-permute-done | bytes 16416 | tf_op jit(solution)/shard_map/ppermute | solution.py:41
  104.1 6.0 %all_gather.3 = bf16[256,256]{1,0:T(8,128)(2,1)} all-gather(bf16[64,256]{1,0:T(8,128)(2,1)S(1)} %copy-done.5), channel_id=1, replica_groups=mesh['prow'=4,'pcol'=8] {'prow'}, dimensions={0}, use_global_device_ids=true | all-gather | bytes 163840 | tf_op jit(solution)/shard_map/all_gather | solution.py:38
  118.9 40.7 %gather_fusion.11 = bf16[4096,256]{1,0:T(8,128)(2,1)} fusion(bf16[16,256,256]{2,1,0:T(8,128)(2,1)S(1)} %gather_fusion.6, s32[4096]{0:T(1024)S(1)} %bitcast.105), kind=kCustom, calls=%fused_computation.11 | custom fusion | bytes 4227072 | tf_op jit(solution)/shard_map/vmap()/gather | solution.py:19
  161.7 16.0 %copy_select_fusion = (bf16[16,256,256]{2,0,1:T(8,128)(2,1)}, bf16[16,256,256]{2,0,1:T(8,128)(2,1)S(1)}) fusion(bf16[16,256,256]{2,1,0:T(8,128)(2,1)} %gather_fusion.3, pred[16]{0:T(512)(128)(4,1)S(1)} %iota_compare_fusion.1, pred[16]{0:T(512)(128)(4,1)S(1)} %get-tuple-element.155, bf16[1,1,16,256,256]{4,3,2,1,0:T(8,128)(2,1)S(1)} %copy-done.1, ...), kind=kLoop, calls=%fused_computation.27 | loop fusion | flops 4194304 | bytes 12587056 | tf_op jit(solution)/shard_map/jit(_where)/select_n | solution.py:105
  177.7 2.1 copy.82
  179.8 2.2 gather_fusion.8
  182.0 2.1 copy.84
  184.1 2.2 gather_fusion.9
  189.4 2.4 scatter_fusion
  191.8 67.9 %all-reduce.4.cloned.1.call-done = bf16[3,256,256]{2,1,0:T(8,128)(2,1)} async-done(((bf16[3,256,256]{2,1,0:T(8,128)(2,1)}), bf16[3,256,256]{2,1,0:T(8,128)(2,1)}) %all-reduce.4.cloned.1.call-update) | async-done | bytes 393232 | tf_op jit(solution)/shard_map/psum | solution.py:15
  259.7 111.2 %while.11 = (s32[]{:T(128)}, bf16[16,256,256]{2,1,0:T(8,128)(2,1)}, s32[]{:T(128)}, s32[16]{0:T(128)S(1)}, bf16[16,256,256]{2,1,0:T(8,128)(2,1)}, /*index=5*/s32...) while((s32[]{:T(128)}, bf16[16,256,256]{2,1,0:T(8,128)(2,1)}, ...), condition=%wide.region_18.19_spmd, body=%wide.region_16.18_spmd.sunk | while | flops 33816608 | bytes 656726 | solution.py:122
  269.4 2.6 fusion.51
  281.7 2.6 fusion.51
  294.0 2.6 fusion.51
  306.3 2.6 fusion.51
  318.5 2.6 fusion.51
  330.8 2.6 fusion.51
  343.1 2.6 fusion.51
  355.4 2.6 fusion.51
  367.7 2.6 fusion.51
  (126 shorter events, 46.8 us)
Async XLA Ops:
  6.5 105.0 %all-reduce.6.cloned.1.call-start = ((), (), s32[]{:S(2)}) async-start(), calls=%async_computation.1 | async-start | bytes 4194304 | tf_op jit(solution)/shard_map/psum | solution.py:59
  7.4 61.5 %collective-permute-start = (bf16[256,32]{1,0:T(8,128)(2,1)S(1)}, bf16[256,32]{1,0:T(8,128)(2,1)S(1)}, u32[]{:S(2)}, u32[]{:S(2)}) collective-permute-start(bf16[256,32]{1,0:T(8,128)(2,1)S(1)} %copy.71), channel_id=1, source_target_pairs={{0,1},{1,2},{2,3},{3,4},{4,5},{5,6},{6,7},{7,0},{8,9},{9,10},{10,1... | collective-permute-start | bytes 49160 | tf_op jit(solution)/shard_map/ppermute | solution.py:41
  11.1 3.0 copy-start.8
  11.1 3.0 copy-start
  14.0 2.4 copy-start.7
  21.7 238.0 %all-reduce.4.cloned.1.call-start = ((), (), s32[]{:S(2)}) async-start(), calls=%async_computation | async-start | bytes 786432 | tf_op jit(solution)/shard_map/psum | solution.py:15
  45.7 58.4 %copy-start.5 = (bf16[64,256]{1,0:T(8,128)(2,1)S(1)}, bf16[64,256]{1,0:T(8,128)(2,1)}, u32[]{:S(2)}) copy-start(bf16[64,256]{1,0:T(8,128)(2,1)} %param.15) | copy-start | bytes 98308
  68.9 7.0 %collective-permute-start.1 = (bf16[256,32]{1,0:T(8,128)(2,1)S(1)}, bf16[256,32]{1,0:T(8,128)(2,1)S(1)}, u32[]{:S(2)}, u32[]{:S(2)}) collective-permute-start(bf16[256,32]{1,0:T(8,128)(2,1)S(1)} %collective-permute-done), channel_id=1, source_target_pairs={{0,1},{1,2},{2,3},{3,4},{4,5},{5,6},{6,7},{7,0},{8,9},{9,10},{10,1... | collective-permute-start | bytes 49160 | tf_op jit(solution)/shard_map/ppermute | solution.py:41
  75.9 7.0 %collective-permute-start.2 = (bf16[256,32]{1,0:T(8,128)(2,1)S(1)}, bf16[256,32]{1,0:T(8,128)(2,1)S(1)}, u32[]{:S(2)}, u32[]{:S(2)}) collective-permute-start(bf16[256,32]{1,0:T(8,128)(2,1)S(1)} %collective-permute-done.1), channel_id=1, source_target_pairs={{0,1},{1,2},{2,3},{3,4},{4,5},{5,6},{6,7},{7,0},{8,9},{9,10},{10,1... | collective-permute-start | bytes 49160 | tf_op jit(solution)/shard_map/ppermute | solution.py:41
  82.8 7.3 %collective-permute-start.3 = (bf16[256,32]{1,0:T(8,128)(2,1)S(1)}, bf16[256,32]{1,0:T(8,128)(2,1)S(1)}, u32[]{:S(2)}, u32[]{:S(2)}) collective-permute-start(bf16[256,32]{1,0:T(8,128)(2,1)S(1)} %collective-permute-done.2), channel_id=1, source_target_pairs={{0,1},{1,2},{2,3},{3,4},{4,5},{5,6},{6,7},{7,0},{8,9},{9,10},{10,1... | collective-permute-start | bytes 49160 | tf_op jit(solution)/shard_map/ppermute | solution.py:41
  90.1 7.0 %collective-permute-start.4 = (bf16[256,32]{1,0:T(8,128)(2,1)S(1)}, bf16[256,32]{1,0:T(8,128)(2,1)S(1)}, u32[]{:S(2)}, u32[]{:S(2)}) collective-permute-start(bf16[256,32]{1,0:T(8,128)(2,1)S(1)} %collective-permute-done.3), channel_id=1, source_target_pairs={{0,1},{1,2},{2,3},{3,4},{4,5},{5,6},{6,7},{7,0},{8,9},{9,10},{10,1... | collective-permute-start | bytes 49160 | tf_op jit(solution)/shard_map/ppermute | solution.py:41
  97.1 7.0 %collective-permute-start.5 = (bf16[256,32]{1,0:T(8,128)(2,1)S(1)}, bf16[256,32]{1,0:T(8,128)(2,1)S(1)}, u32[]{:S(2)}, u32[]{:S(2)}) collective-permute-start(bf16[256,32]{1,0:T(8,128)(2,1)S(1)} %collective-permute-done.4), channel_id=1, source_target_pairs={{0,1},{1,2},{2,3},{3,4},{4,5},{5,6},{6,7},{7,0},{8,9},{9,10},{10,1... | collective-permute-start | bytes 49160 | tf_op jit(solution)/shard_map/ppermute | solution.py:41
  104.1 7.0 %collective-permute-start.6 = (bf16[256,32]{1,0:T(8,128)(2,1)S(1)}, bf16[256,32]{1,0:T(8,128)(2,1)S(1)}, u32[]{:S(2)}, u32[]{:S(2)}) collective-permute-start(bf16[256,32]{1,0:T(8,128)(2,1)S(1)} %collective-permute-done.5), channel_id=1, source_target_pairs={{0,1},{1,2},{2,3},{3,4},{4,5},{5,6},{6,7},{7,0},{8,9},{9,10},{10,1... | collective-permute-start | bytes 49160 | tf_op jit(solution)/shard_map/ppermute | solution.py:41
  111.6 1.5 copy-start.3
  159.7 2.0 copy-start.1
  177.7 4.3 %copy-start.2 = (bf16[16,256,256]{2,0,1:T(8,128)(2,1)S(1)}, bf16[16,256,256]{2,0,1:T(8,128)(2,1)}, u32[]{:S(2)}) copy-start(bf16[16,256,256]{2,0,1:T(8,128)(2,1)} %get-tuple-element.145) | copy-start | bytes 6291460
  182.0 4.3 %copy-start.4 = (bf16[256,256]{1,0:T(8,128)(2,1)S(1)}, bf16[256,256]{1,0:T(8,128)(2,1)}, u32[]{:S(2)}) copy-start(bf16[256,256]{1,0:T(8,128)(2,1)} %all_gather.3) | copy-start | bytes 393220
  184.1 75.6 %copy-start.6 = (s32[3]{0:T(128)S(1)}, s32[3]{0:T(128)}, u32[]{:S(2)}) copy-start(s32[3]{0:T(128)} %constant.124.clone.1) | copy-start | bytes 40
Sparse Core Ops, SparseCore 0:
  21.9 51.7 all-reduce.5
  187.4 72.2 all-reduce.3
